TPU v7x, 32 devices: a whole 2x2x4 slice. The times are simulated.
32 devices in a mesh: groups: 2 (over y), grid: 4 (over z), depth: 4 (over x, core).
Axes of the slice: x: 2, y: 2, z: 4, core: 2. Of those that a mesh axis runs over, the one named last changes fastest.
Arguments:
- tokens: bfloat16 [512, 4096], P(('groups', 'grid'), 'depth'), parts along dimension 0, may hold values from -6 to 6
- gate_weight: bfloat16 [4096, 14336], P('depth', 'grid'), may hold values from -0.09375 to 0.09375
- up_weight: bfloat16 [4096, 14336], P('depth', 'grid'), may hold values from -0.09375 to 0.09375
- down_weight: bfloat16 [14336, 4096], P('grid', 'depth'), may hold values from -0.046875 to 0.046875
Outputs:
- mixed: bfloat16 [512, 4096], P(('groups', 'grid'), 'depth'), parts along dimension 0
There are 2 independent parts, one for each index of `groups`. A program takes and returns all parts, laid end to end along the dimension named above; an argument that names none is the same for every part. Nothing has to cross between parts.
All inputs are finite; a program needn't handle non-finite values.
Results may differ from a plain program's by a relative error of at most 0.0049.
Values may be sent and summed in bfloat16 or wider, within the bound.
A program may use at most 64 MiB of HBM per device.

v0:
```python
import functools

import jax
import jax.numpy as jnp
from jax import lax
from jax.experimental import pallas as pl
from jax.experimental.pallas import tpu as pltpu
from jax.sharding import PartitionSpec as P

MESH = pl.DeviceIdType.MESH
LAG_SUM, LAG_HID, LAG_FWD, LAG_OUT = 1, 4, 7, 9
HEAD = 5
SLOTS = 8


def flip(index, mask):
    out, bit = index, 1
    while bit <= mask:
        if mask & bit:
            out = out + bit - 2 * bit * lax.rem(lax.div(index, bit), 2)
        bit *= 2
    return out


def kernel(n, chunks, width, tokens, gate_w, up_w, down_w, out, tok, gate_v, up_v, down_v, part, core_out, core_in,
           keep, chip_out, chip_in, hid, acc, grid_out, grid_in,
           w_sem, d_sem, tok_sem, toks_sem, tokr_sem, cores_sem, corer_sem, chips_sem, chipr_sem,
           hids_sem, hidr_sem, fwds_sem, fwdr_sem, grids_sem, gridr_sem):
    z, depth = lax.axis_index("grid"), lax.axis_index("depth")
    a, b = lax.div(depth, 2), lax.rem(depth, 2)
    other_core, other_chip = {"depth": depth + 1 - 2 * b}, {"depth": depth + 2 - 4 * a}
    peers = [{"grid": flip(z, mask)} for mask in range(n)]
    rows = tok.shape[1]
    half, quarter = rows // 2, rows // 4
    my_half = pl.ds(pl.multiple_of(b * half, half), half)
    their_half = pl.ds(pl.multiple_of((1 - b) * half, half), half)
    my_rows = pl.ds(pl.multiple_of(b * half + a * quarter, quarter), quarter)
    their_rows = pl.ds(pl.multiple_of(b * half + (1 - a) * quarter, quarter), quarter)
    keep_rows = pl.ds(pl.multiple_of(a * quarter, quarter), quarter)
    give_rows = pl.ds(pl.multiple_of((1 - a) * quarter, quarter), quarter)
    units = n * chunks
    head = min(HEAD, chunks)
    ahead = chunks - head
    order = [k % chunks for k in range(ahead, ahead + chunks)]

    def columns(k):
        return pl.ds(k * width if isinstance(k, int) else pl.multiple_of(k * width, width), width)

    own = pltpu.make_async_copy(tokens, tok.at[0], tok_sem)
    own.start()
    def load(k):
        pltpu.make_async_copy(gate_w.at[:, columns(k)], gate_v.at[k], w_sem.at[2 * k]).start()
        pltpu.make_async_copy(up_w.at[:, columns(k)], up_v.at[k], w_sem.at[2 * k + 1]).start()

    for j in range(min(2, chunks)):
        load((ahead + j) % chunks)

    barrier = pltpu.get_barrier_semaphore()
    for peer in [other_core, other_chip] + peers[1:]:
        pl.semaphore_signal(barrier, inc=1, device_id=peer, device_id_type=MESH)
    pl.semaphore_wait(barrier, n + 1)
    own.wait()

    def tok_copy(s):
        return pltpu.make_async_remote_copy(
            tok.at[0], tok.at[s], toks_sem.at[s], tokr_sem.at[s], device_id=peers[s], device_id_type=MESH)

    def core_copy(i):
        return pltpu.make_async_remote_copy(
            core_out.at[i], core_in.at[i], cores_sem, corer_sem.at[i], device_id=other_core, device_id_type=MESH)

    def chip_copy(i):
        return pltpu.make_async_remote_copy(
            chip_out.at[i], chip_in.at[i], chips_sem, chipr_sem.at[i], device_id=other_chip, device_id_type=MESH)

    def hid_copy(i, at):
        return pltpu.make_async_remote_copy(
            hid.at[i, at], hid.at[i, at], hids_sem, hidr_sem.at[i], device_id=other_chip, device_id_type=MESH)

    def fwd_copy(i, at):
        return pltpu.make_async_remote_copy(
            hid.at[i, at], hid.at[i, at], fwds_sem, fwdr_sem.at[i], device_id=other_core, device_id_type=MESH)

    def grid_copy(s):
        return pltpu.make_async_remote_copy(
            grid_out.at[s], grid_in.at[s], grids_sem.at[s], gridr_sem.at[s], device_id=peers[s], device_id_type=MESH)

    for s in range(1, n):
        tok_copy(s).start()

    acc[...] = jnp.zeros_like(acc)

    def step(t, carry):
        @pl.when(t + 2 < chunks)
        def _():
            load(lax.rem(t + ahead + 2, chunks))

        @pl.when(jnp.logical_and(t >= 6, t < chunks + 6))
        def _():
            k = lax.rem(t - 6 + ahead, chunks)
            pltpu.make_async_copy(down_w.at[columns(k), :], down_v.at[k], d_sem.at[k]).start()

        @pl.when(t < units)
        def _():
            i = t
            s, k, slot = lax.rem(lax.div(i + ahead, chunks), n), lax.rem(i + ahead, chunks), lax.rem(i, SLOTS)
            for c in range(1, n):
                @pl.when(i == c * chunks - ahead)
                def _():
                    tok_copy(c).wait_recv()

            @pl.when(i < chunks)
            def _():
                pltpu.make_async_copy(gate_w.at[:, pl.ds(0, width)], gate_v.at[k], w_sem.at[2 * k]).wait()
                pltpu.make_async_copy(up_w.at[:, pl.ds(0, width)], up_v.at[k], w_sem.at[2 * k + 1]).wait()

            x = tok[s]
            part[slot, :, :width] = jnp.dot(x, gate_v[k], preferred_element_type=jnp.float32)
            part[slot, :, width:] = jnp.dot(x, up_v[k], preferred_element_type=jnp.float32)
            core_out[i] = part[slot, their_half, :]
            core_copy(i).start()

        @pl.when(jnp.logical_and(t >= LAG_SUM, t < units + LAG_SUM))
        def _():
            i = t - LAG_SUM
            slot = lax.rem(i, SLOTS)
            core_copy(i).wait_recv()
            give = pl.ds(pl.multiple_of(b * half + (1 - a) * quarter, quarter), quarter)
            chip_out[i] = (part[slot, give, :] + core_in[i, give_rows, :]).astype(jnp.bfloat16)
            chip_copy(i).start()
            keep[lax.rem(i, SLOTS)] = part[slot, my_rows, :] + core_in[i, keep_rows, :]

        @pl.when(jnp.logical_and(t >= LAG_HID, t < units + LAG_HID))
        def _():
            i = t - LAG_HID
            chip_copy(i).wait_recv()
            summed = keep[lax.rem(i, SLOTS)] + chip_in[i].astype(jnp.float32)
            g, u = summed[:, :width], summed[:, width:]
            hid[i, my_rows, :] = (g / (1.0 + jnp.exp(-g)) * u).astype(jnp.bfloat16)
            hid_copy(i, my_rows).start()

        @pl.when(jnp.logical_and(t >= LAG_FWD, t < units + LAG_FWD))
        def _():
            i = t - LAG_FWD
            hid_copy(i, their_rows).wait_recv()
            fwd_copy(i, my_half).start()

        @pl.when(t >= LAG_OUT)
        def _():
            i = t - LAG_OUT
            s, k = lax.rem(lax.div(i + ahead, chunks), n), lax.rem(i + ahead, chunks)

            @pl.when(i < chunks)
            def _():
                pltpu.make_async_copy(down_w.at[pl.ds(0, width), :], down_v.at[k], d_sem.at[k]).wait()

            fwd_copy(i, their_half).wait_recv()

            acc[s] += jnp.dot(hid[i], down_v[k], preferred_element_type=jnp.float32)

            for c in range(1, n):
                @pl.when(i == c * chunks + head - 1)
                def _():
                    grid_out[c] = acc[c].astype(jnp.bfloat16)
                    grid_copy(c).start()

        return carry

    lax.fori_loop(0, units + LAG_OUT, step, 0)

    total = acc[0]
    for s in range(1, n):
        grid_copy(s).wait_recv()
        total = total + grid_in[s].astype(jnp.float32)
    out[...] = total.astype(out.dtype)

    for s in range(1, n):
        tok_copy(s).wait_send()
        grid_copy(s).wait_send()

    def drain(ref, sem, device):
        pltpu.make_async_remote_copy(
            ref, ref, sem, corer_sem.at[0], device_id=device, device_id_type=MESH).wait_send()

    drain(core_out, cores_sem, other_core)
    drain(chip_out, chips_sem, other_chip)
    drain(hid.at[:, my_rows], hids_sem, other_chip)
    drain(hid.at[:, my_half], fwds_sem, other_core)


def fused(n, width, tokens, gate_weight, up_weight, down_weight):
    rows, feats = tokens.shape
    share, outs = down_weight.shape
    chunks = share // width
    units = n * chunks
    vmem, dma = pltpu.VMEM, pltpu.SemaphoreType.DMA
    bf, f4 = jnp.bfloat16, jnp.float32
    return pl.pallas_call(
        functools.partial(kernel, n, chunks, width),
        out_shape=jax.ShapeDtypeStruct((rows, outs), bf),
        in_specs=[pl.BlockSpec(memory_space=pl.ANY)] * 4,
        out_specs=pl.BlockSpec(memory_space=pltpu.VMEM),
        scratch_shapes=[
            vmem((n, rows, feats), bf),
            vmem((chunks, feats, width), bf),
            vmem((chunks, feats, width), bf),
            vmem((chunks, width, outs), bf),
            vmem((SLOTS, rows, 2 * width), f4),
            vmem((units, rows // 2, 2 * width), f4),
            vmem((units, rows // 2, 2 * width), f4),
            vmem((SLOTS, rows // 4, 2 * width), f4),
            vmem((units, rows // 4, 2 * width), bf),
            vmem((units, rows // 4, 2 * width), bf),
            vmem((units, rows, width), bf),
            vmem((n, rows, outs), f4),
            vmem((n, rows, outs), bf),
            vmem((n, rows, outs), bf),
            dma((2 * chunks,)), dma((chunks,)), dma, dma((n,)), dma((n,)),
            dma, dma((units,)), dma, dma((units,)),
            dma, dma((units,)), dma, dma((units,)), dma((n,)), dma((n,)),
        ],
        compiler_params=pltpu.CompilerParams(
            collective_id=0, has_side_effects=True, vmem_limit_bytes=60 * 1024 * 1024),
    )(tokens, gate_weight, up_weight, down_weight)


def plain(tokens, gate_weight, up_weight, down_weight):
    grid_size = lax.axis_size("grid")
    block_rows = tokens.shape[0]
    total_rows = block_rows * grid_size
    width_share = gate_weight.shape[1]
    stacked = jnp.concatenate([gate_weight, up_weight], axis=1)
    pre_act = jnp.dot(
        lax.all_gather(tokens, "grid", axis=0, tiled=True), stacked, preferred_element_type=jnp.float32)
    blocked = pre_act.reshape(grid_size, block_rows, 2 * width_share)
    summed = lax.psum_scatter(blocked, "depth", scatter_dimension=1, tiled=True)
    hidden = lax.all_gather(
        (jax.nn.silu(summed[..., :width_share]) * summed[..., width_share:]).astype(jnp.bfloat16),
        "depth", axis=1, tiled=True,
    ).reshape(total_rows, width_share)
    return lax.psum_scatter(
        jnp.dot(hidden, down_weight, preferred_element_type=jnp.float32),
        "grid", scatter_dimension=0, tiled=True,
    ).astype(jnp.bfloat16)


def body(tokens, gate_weight, up_weight, down_weight):
    n, depth = lax.axis_size("grid"), lax.axis_size("depth")
    rows, share = tokens.shape[0], gate_weight.shape[1]
    width = next((w for w in (512, 256) if share % w == 0), None)
    weights = 2 * (2 * gate_weight.size + down_weight.size)
    if depth == 4 and n in (2, 4, 8) and rows == 64 and width and weights < 32 * 2**20:
        return fused(n, width, tokens, gate_weight, up_weight, down_weight)
    return plain(tokens, gate_weight, up_weight, down_weight)


def solution(mesh):
    placed = (
        P(("groups", "grid"), "depth"),
        P("depth", "grid"),
        P("depth", "grid"),
        P("grid", "depth"),
    )
    return jax.shard_map(
        body, mesh=mesh, in_specs=placed, out_specs=P(("groups", "grid"), "depth"), check_vma=False
    )
```

profile of v0, /device:TPU:0, one launch (start us, length us, event | category | flops | bytes accessed | tf_op | source)
XLA Modules:
  0.0 51.6 jit_solution(15297399536110917637)
XLA Ops:
  0.0 50.0 %shard_map.46 = bf16[64,1024]{1,0:T(8,128)(2,1)} custom-call(bf16[64,1024]{1,0:T(8,128)(2,1)} %tokens.1, bf16[1024,3584]{1,0:T(8,128)(2,1)} %gate_w.1, bf16[1024,3584]{1,0:T(8,128)(2,1)} %up_w.1, bf16[3584,1024]{1,0:T(8,128)(2,1)} %down_w.1), custom_call_target="tpu_custom_call" | custom-call | tf_op jit(solution)/shard_map/pallas_call | solution.py:198
  50.0 1.6 %copy.6 = bf16[64,1024]{1,0:T(8,128)(2,1)} copy(bf16[64,1024]{1,0:T(8,128)(2,1)} %shard_map.46) | data formatting | bytes 262144
where the time goes:
time: 51.7 us; the launch traced here: 51.6 us
  Pallas kernels  50 us (97%)
  local copies, waits for them, and re-layouts  1.57 us (3%)
    pallas_call x1, Pallas kernels, fused(): pl.pallas_call(functools.partial(kernel, n, chunks, width), out_shape=jax...  50 us
    unnamed x1, local copies, waits for them, and re-layouts  1.57 us

commit v1 on v0

v1 whole, which is shorter than its diff:
```python
import functools

import jax
import jax.numpy as jnp
from jax import lax
from jax.experimental import pallas as pl
from jax.experimental.pallas import tpu as pltpu
from jax.sharding import PartitionSpec as P

MESH = pl.DeviceIdType.MESH
FILL = (0, 3, 6, 9, 11)
STEADY = (0, 3, 6, 9, 11)
HEAD, NEXT, GAP = 5, 2, 0
DOWN_AT = 6


def flip(index, mask):
    out, bit = index, 1
    while bit <= mask:
        if mask & bit:
            out = out + bit - 2 * bit * lax.rem(lax.div(index, bit), 2)
        bit *= 2
    return out


def kernel(n, chunks, width, tokens, gate_w, up_w, down_w, out, tok, gate_v, up_v, down_v, part, core_out, core_in,
           chip_out, chip_in, hid, acc, grid_out, grid_in,
           w_sem, d_sem, tok_sem, toks_sem, tokr_sem, cores_sem, corer_sem, chips_sem, chipr_sem,
           hids_sem, hidr_sem, fwds_sem, fwdr_sem, grids_sem, gridr_sem):
    z, depth = lax.axis_index("grid"), lax.axis_index("depth")
    a, b = lax.div(depth, 2), lax.rem(depth, 2)
    other_core, other_chip = {"depth": depth + 1 - 2 * b}, {"depth": depth + 2 - 4 * a}
    peers = [{"grid": flip(z, mask)} for mask in [0, 1] + list(range(n - 1, 1, -1))]
    rows = tok.shape[1]
    half, quarter = rows // 2, rows // 4

    def span(core, chip):
        return pl.ds(pl.multiple_of(core * half + chip * quarter, quarter), quarter)

    my_rows, chip_rows = span(b, a), span(b, 1 - a)
    their_half = pl.ds(pl.multiple_of((1 - b) * half, half), half)
    sent = [my_rows, chip_rows, span(1 - b, a), span(1 - b, 1 - a)]
    units = n * chunks
    head = min(HEAD, chunks)
    ahead = chunks - head
    near = min(NEXT, chunks)
    filled = head + near
    back, last = filled + (n - 2) * chunks, head + (n - 1) * chunks
    entry = [0, head] + [filled + (c - 2) * chunks for c in range(2, n)]
    leave = [0, last - 1 if near < chunks else filled - 1] + [filled + (c - 1) * chunks - 1 for c in range(2, n)]

    def columns(k):
        return pl.ds(k * width if isinstance(k, int) else pl.multiple_of(k * width, width), width)

    def place(i):
        far = 2 + lax.div(jnp.maximum(i - filled, 0), chunks)
        s = jnp.where(i < head, 0, jnp.where(i < filled, 1, jnp.where(i < back, far, jnp.where(i < last, 1, 0))))
        return s, lax.rem(i + ahead, chunks)

    own = pltpu.make_async_copy(tokens, tok.at[0], tok_sem)
    own.start()

    def load(k):
        pltpu.make_async_copy(gate_w.at[:, columns(k)], gate_v.at[k], w_sem.at[2 * k]).start()
        pltpu.make_async_copy(up_w.at[:, columns(k)], up_v.at[k], w_sem.at[2 * k + 1]).start()

    for j in range(min(2, chunks)):
        load((ahead + j) % chunks)

    barrier = pltpu.get_barrier_semaphore()
    for peer in [other_core, other_chip] + peers[1:]:
        pl.semaphore_signal(barrier, inc=1, device_id=peer, device_id_type=MESH)
    acc[...] = jnp.zeros_like(acc)

    def tok_copy(s):
        return pltpu.make_async_remote_copy(
            tok.at[0], tok.at[s], toks_sem.at[s], tokr_sem.at[s], device_id=peers[s], device_id_type=MESH)

    def core_copy(i):
        return pltpu.make_async_remote_copy(
            core_out.at[i], core_in.at[i], cores_sem, corer_sem.at[i], device_id=other_core, device_id_type=MESH)

    def chip_copy(i):
        return pltpu.make_async_remote_copy(
            chip_out.at[i], chip_in.at[i], chips_sem, chipr_sem.at[i], device_id=other_chip, device_id_type=MESH)

    def hid_copy(i, at):
        return pltpu.make_async_remote_copy(
            hid.at[i, at], hid.at[i, at], hids_sem, hidr_sem.at[i], device_id=other_chip, device_id_type=MESH)

    def fwd_copy(i, at):
        return pltpu.make_async_remote_copy(
            hid.at[i, at], hid.at[i, at], fwds_sem, fwdr_sem.at[i], device_id=other_core, device_id_type=MESH)

    def grid_copy(s):
        return pltpu.make_async_remote_copy(
            grid_out.at[s], grid_in.at[s], grids_sem.at[s], gridr_sem.at[s], device_id=peers[s], device_id_type=MESH)

    def started():
        pl.semaphore_wait(barrier, n + 1)
        own.wait()
        for s in range(1, max(n - 1, 2)):
            tok_copy(s).start()

    def ready(t):
        s, k = place(t)
        for c in range(1, n):
            @pl.when(t == entry[c])
            def _():
                tok_copy(c).wait_recv()
                if c == 1 and n > 2:
                    tok_copy(n - 1).start()

        @pl.when(t < chunks)
        def _():
            pltpu.make_async_copy(gate_w.at[:, pl.ds(0, width)], gate_v.at[k], w_sem.at[2 * k]).wait()
            pltpu.make_async_copy(up_w.at[:, pl.ds(0, width)], up_v.at[k], w_sem.at[2 * k + 1]).wait()

    def project(t):
        s, k = place(t)
        x = jnp.concatenate([tok[s, at, :] for at in sent], axis=0)
        gate = jnp.dot(x, gate_v[k], preferred_element_type=jnp.float32)
        part[t, :, :width] = gate[:half]
        core_out[t, :, :width] = gate[half:]
        up = jnp.dot(x, up_v[k], preferred_element_type=jnp.float32)
        part[t, :, width:] = up[:half]
        core_out[t, :, width:] = up[half:]

    def reduce_core(i):
        chip_out[i] = (part[i, quarter:] + core_in[i, quarter:]).astype(jnp.bfloat16)

    def activate(i):
        summed = part[i, :quarter] + core_in[i, :quarter] + chip_in[i].astype(jnp.float32)
        g, u = summed[:, :width], summed[:, width:]
        hid[i, my_rows, :] = (g / (1.0 + jnp.exp(-g)) * u).astype(jnp.bfloat16)

    def down(i):
        s, k = place(i)
        acc[s] += jnp.dot(hid[i], down_v[k], preferred_element_type=jnp.float32)

    def step(offsets, loads, t, carry):
        dot, red, act, fwd, dwn = [None if o is None else t + o for o in offsets]
        if dot is not None:
            @pl.when(dot + 2 < chunks)
            def _():
                load(lax.rem(dot + ahead + 2, chunks))
        if loads:
            @pl.when(jnp.logical_and(t >= DOWN_AT, t < chunks + DOWN_AT))
            def _():
                k = lax.rem(t - DOWN_AT + ahead, chunks)
                pltpu.make_async_copy(down_w.at[columns(k), :], down_v.at[k], d_sem.at[k]).start()
        if red is not None:
            core_copy(red).wait_recv()
            reduce_core(red)
            chip_copy(red).start()
        if act is not None:
            chip_copy(act).wait_recv()
            activate(act)
            hid_copy(act, my_rows).start()
            fwd_copy(act, my_rows).start()
        if fwd is not None:
            hid_copy(fwd, chip_rows).wait_recv()
            fwd_copy(fwd, chip_rows).start()
        if dwn is not None:
            k = place(dwn)[1]

            @pl.when(dwn < chunks)
            def _():
                pltpu.make_async_copy(down_w.at[pl.ds(0, width), :], down_v.at[k], d_sem.at[k]).wait()

            fwd_copy(dwn, their_half).wait_recv()
        if dot is not None:
            ready(dot)
            project(dot)
        if dwn is not None:
            down(dwn)
        if dot is not None:
            core_copy(dot).start()
        if dwn is not None:
            for c in range(1, n):
                @pl.when(dwn == leave[c])
                def _():
                    grid_out[c] = acc[c].astype(jnp.bfloat16)
                    grid_copy(c).start()
        return carry

    started()
    plan = {}
    for i in range(units):
        for stage, lag in enumerate(FILL if i < filled else STEADY):
            t = i + lag + (0 if i < filled else GAP)
            plan.setdefault(t, [None] * 5)[stage] = i - t
    steps = [tuple(plan.get(t, [None] * 5)) for t in range(max(plan) + 1)]
    low = 0
    for t in range(1, len(steps) + 1):
        if t == len(steps) or steps[t] != steps[low]:
            loads = low < chunks + DOWN_AT and t > DOWN_AT
            lax.fori_loop(low, t, functools.partial(step, steps[low], loads), 0)
            low = t

    total = acc[0]
    for s in range(1, n):
        grid_copy(s).wait_recv()
        total = total + grid_in[s].astype(jnp.float32)
    out[...] = total.astype(out.dtype)

    for s in range(1, n):
        tok_copy(s).wait_send()
        grid_copy(s).wait_send()

    def drain(ref, sem, device):
        pltpu.make_async_remote_copy(
            ref, ref, sem, corer_sem.at[0], device_id=device, device_id_type=MESH).wait_send()

    drain(core_out, cores_sem, other_core)
    drain(chip_out, chips_sem, other_chip)
    drain(hid.at[:, my_rows], hids_sem, other_chip)
    drain(hid.at[:, their_half], fwds_sem, other_core)


def fused(n, width, tokens, gate_weight, up_weight, down_weight):
    rows, feats = tokens.shape
    share, outs = down_weight.shape
    chunks = share // width
    units = n * chunks
    vmem, dma = pltpu.VMEM, pltpu.SemaphoreType.DMA
    bf, f4 = jnp.bfloat16, jnp.float32
    return pl.pallas_call(
        functools.partial(kernel, n, chunks, width),
        out_shape=pltpu.VMEM((rows, outs), bf),
        in_specs=[pl.BlockSpec(memory_space=pl.ANY)] * 4,
        out_specs=pl.BlockSpec(memory_space=pltpu.VMEM),
        scratch_shapes=[
            vmem((n, rows, feats), bf),
            vmem((chunks, feats, width), bf),
            vmem((chunks, feats, width), bf),
            vmem((chunks, width, outs), bf),
            vmem((units, rows // 2, 2 * width), f4),
            vmem((units, rows // 2, 2 * width), f4),
            vmem((units, rows // 2, 2 * width), f4),
            vmem((units, rows // 4, 2 * width), bf),
            vmem((units, rows // 4, 2 * width), bf),
            vmem((units, rows, width), bf),
            vmem((n, rows, outs), f4),
            vmem((n, rows, outs), bf),
            vmem((n, rows, outs), bf),
            dma((2 * chunks,)), dma((chunks,)), dma, dma((n,)), dma((n,)),
            dma, dma((units,)), dma, dma((units,)),
            dma, dma((units,)), dma, dma((units,)), dma((n,)), dma((n,)),
        ],
        compiler_params=pltpu.CompilerParams(
            collective_id=0, has_side_effects=True, vmem_limit_bytes=60 * 1024 * 1024),
    )(tokens, gate_weight, up_weight, down_weight)


def plain(tokens, gate_weight, up_weight, down_weight):
    grid_size = lax.axis_size("grid")
    block_rows = tokens.shape[0]
    total_rows = block_rows * grid_size
    width_share = gate_weight.shape[1]
    stacked = jnp.concatenate([gate_weight, up_weight], axis=1)
    pre_act = jnp.dot(
        lax.all_gather(tokens, "grid", axis=0, tiled=True), stacked, preferred_element_type=jnp.float32)
    blocked = pre_act.reshape(grid_size, block_rows, 2 * width_share)
    summed = lax.psum_scatter(blocked, "depth", scatter_dimension=1, tiled=True)
    hidden = lax.all_gather(
        (jax.nn.silu(summed[..., :width_share]) * summed[..., width_share:]).astype(jnp.bfloat16),
        "depth", axis=1, tiled=True,
    ).reshape(total_rows, width_share)
    return lax.psum_scatter(
        jnp.dot(hidden, down_weight, preferred_element_type=jnp.float32),
        "grid", scatter_dimension=0, tiled=True,
    ).astype(jnp.bfloat16)


def body(tokens, gate_weight, up_weight, down_weight):
    n, depth = lax.axis_size("grid"), lax.axis_size("depth")
    rows, share = tokens.shape[0], gate_weight.shape[1]
    width = next((w for w in (512, 256) if share % w == 0), None)
    weights = 2 * (2 * gate_weight.size + down_weight.size)
    if depth == 4 and n in (2, 4, 8) and rows == 64 and width and weights < 32 * 2**20:
        return fused(n, width, tokens, gate_weight, up_weight, down_weight)
    return plain(tokens, gate_weight, up_weight, down_weight)


def solution(mesh):
    placed = (
        P(("groups", "grid"), "depth"),
        P("depth", "grid"),
        P("depth", "grid"),
        P("grid", "depth"),
    )
    return jax.shard_map(
        body, mesh=mesh, in_specs=placed, out_specs=P(("groups", "grid"), "depth"), check_vma=False
    )
```

time: 51.7 us -> 48.9 us (0.946)
  Pallas kernels: 50 us -> 48.1 us
  local copies, waits for them, and re-layouts: 1.57 us -> 0.66 us
    pallas_call x1, Pallas kernels: 50 us -> 48.1 us  [fused(): pl.pallas_call(functools.partial(kernel, n, chunks, width), out_shape=plt...]
    unnamed x1, local copies, waits for them, and re-layouts: 1.57 us -> 0.66 us
where the time goes in v1:
time: 48.9 us; the launch traced here: 48.8 us
  Pallas kernels  48.1 us (98%)
  local copies, waits for them, and re-layouts  0.66 us (1%)
    pallas_call x1, Pallas kernels, fused(): pl.pallas_call(functools.partial(kernel, n, chunks, width), out_shape=plt...  48.1 us

profile of v1, /device:TPU:0, one launch (start us, length us, event | category | flops | bytes accessed | tf_op | source)
XLA Modules:
  0.0 48.8 jit_solution(7320171118145975687)
XLA Ops:
  0.0 48.1 %shard_map.46 = bf16[64,1024]{1,0:T(8,128)(2,1)S(1)} custom-call(bf16[64,1024]{1,0:T(8,128)(2,1)} %tokens.1, bf16[1024,3584]{1,0:T(8,128)(2,1)} %gate_w.1, bf16[1024,3584]{1,0:T(8,128)(2,1)} %up_w.1, bf16[3584,1024]{1,0:T(8,128)(2,1)} %down_w.1), custom_call_target="tpu_custom_call" | custom-call | tf_op jit(solution)/shard_map/pallas_call | solution.py:228
  48.1 0.7 %copy.6 = bf16[64,1024]{1,0:T(8,128)(2,1)} copy(bf16[64,1024]{1,0:T(8,128)(2,1)S(1)} %shard_map.46) | data formatting | bytes 262144

commit v2 on v1

--- a/solution.py
+++ b/solution.py
@@ -8,9 +8,10 @@
 from jax.sharding import PartitionSpec as P
 
 MESH = pl.DeviceIdType.MESH
-FILL = (0, 3, 6, 9, 11)
-STEADY = (0, 3, 6, 9, 11)
-HEAD, NEXT, GAP = 5, 2, 0
+LAGS = (0, 3, 6, 9, 11)
+HEAD = 5
+NEAR = (4, 0)
+LAUNCH = (5, 9)
 DOWN_AT = 6
 
 
@@ -43,11 +44,13 @@
     units = n * chunks
     head = min(HEAD, chunks)
     ahead = chunks - head
-    near = min(NEXT, chunks)
+    outer = jnp.logical_or(z == 0, z == n - 1)
+    near = jnp.where(outer, *[min(count, chunks - 1) for count in NEAR])
+    launch = jnp.where(outer, *LAUNCH)
     filled = head + near
     back, last = filled + (n - 2) * chunks, head + (n - 1) * chunks
-    entry = [0, head] + [filled + (c - 2) * chunks for c in range(2, n)]
-    leave = [0, last - 1 if near < chunks else filled - 1] + [filled + (c - 1) * chunks - 1 for c in range(2, n)]
+    entry = [0, jnp.where(near > 0, head, back)] + [filled + (c - 2) * chunks for c in range(2, n)]
+    leave = [0, last - 1] + [filled + (c - 1) * chunks - 1 for c in range(2, n)]
 
     def columns(k):
         return pl.ds(k * width if isinstance(k, int) else pl.multiple_of(k * width, width), width)
@@ -104,12 +107,15 @@
 
     def ready(t):
         s, k = place(t)
+        if n > 2:
+            @pl.when(t == launch)
+            def _():
+                tok_copy(n - 1).start()
+
         for c in range(1, n):
             @pl.when(t == entry[c])
             def _():
                 tok_copy(c).wait_recv()
-                if c == 1 and n > 2:
-                    tok_copy(n - 1).start()
 
         @pl.when(t < chunks)
         def _():
@@ -187,9 +193,8 @@
     started()
     plan = {}
     for i in range(units):
-        for stage, lag in enumerate(FILL if i < filled else STEADY):
-            t = i + lag + (0 if i < filled else GAP)
-            plan.setdefault(t, [None] * 5)[stage] = i - t
+        for stage, lag in enumerate(LAGS):
+            plan.setdefault(i + lag, [None] * 5)[stage] = -lag
     steps = [tuple(plan.get(t, [None] * 5)) for t in range(max(plan) + 1)]
     low = 0
     for t in range(1, len(steps) + 1):

time: 48.9 us -> 47 us (0.961)
  Pallas kernels: 48.1 us -> 46.2 us
    pallas_call x1, Pallas kernels: 48.1 us -> 46.2 us  [fused(): pl.pallas_call(functools.partial(kernel, n, chunks, width), out_shape=plt...]
where the time goes in v2:
time: 47 us; the launch traced here: 46.9 us
  Pallas kernels  46.2 us (98%)
  local copies, waits for them, and re-layouts  0.66 us (1%)
    pallas_call x1, Pallas kernels, fused(): pl.pallas_call(functools.partial(kernel, n, chunks, width), out_shape=plt...  46.2 us

profile of v2, /device:TPU:0, one launch (start us, length us, event | category | flops | bytes accessed | tf_op | source)
XLA Modules:
  0.0 46.9 jit_solution(1329022081946073114)
XLA Ops:
  0.0 46.2 %shard_map.46 = bf16[64,1024]{1,0:T(8,128)(2,1)S(1)} custom-call(bf16[64,1024]{1,0:T(8,128)(2,1)} %tokens.1, bf16[1024,3584]{1,0:T(8,128)(2,1)} %gate_w.1, bf16[1024,3584]{1,0:T(8,128)(2,1)} %up_w.1, bf16[3584,1024]{1,0:T(8,128)(2,1)} %down_w.1), custom_call_target="tpu_custom_call" | custom-call | tf_op jit(solution)/shard_map/pallas_call | solution.py:233
  46.2 0.7 %copy.6 = bf16[64,1024]{1,0:T(8,128)(2,1)} copy(bf16[64,1024]{1,0:T(8,128)(2,1)S(1)} %shard_map.46) | data formatting | bytes 262144

commit v3 on v2

--- a/solution.py
+++ b/solution.py
@@ -13,6 +13,7 @@
 NEAR = (4, 0)
 LAUNCH = (5, 9)
 DOWN_AT = 6
+RING = 12
 
 
 def flip(index, mask):
@@ -81,19 +82,19 @@
 
     def core_copy(i):
         return pltpu.make_async_remote_copy(
-            core_out.at[i], core_in.at[i], cores_sem, corer_sem.at[i], device_id=other_core, device_id_type=MESH)
+            core_out.at[i], core_in.at[i], cores_sem, corer_sem.at[lax.rem(i, RING)], device_id=other_core, device_id_type=MESH)
 
     def chip_copy(i):
         return pltpu.make_async_remote_copy(
-            chip_out.at[i], chip_in.at[i], chips_sem, chipr_sem.at[i], device_id=other_chip, device_id_type=MESH)
+            chip_out.at[i], chip_in.at[i], chips_sem, chipr_sem.at[lax.rem(i, RING)], device_id=other_chip, device_id_type=MESH)
 
     def hid_copy(i, at):
         return pltpu.make_async_remote_copy(
-            hid.at[i, at], hid.at[i, at], hids_sem, hidr_sem.at[i], device_id=other_chip, device_id_type=MESH)
+            hid.at[i, at], hid.at[i, at], hids_sem, hidr_sem.at[lax.rem(i, RING)], device_id=other_chip, device_id_type=MESH)
 
     def fwd_copy(i, at):
         return pltpu.make_async_remote_copy(
-            hid.at[i, at], hid.at[i, at], fwds_sem, fwdr_sem.at[i], device_id=other_core, device_id_type=MESH)
+            hid.at[i, at], hid.at[i, at], fwds_sem, fwdr_sem.at[lax.rem(i, RING)], device_id=other_core, device_id_type=MESH)
 
     def grid_copy(s):
         return pltpu.make_async_remote_copy(
@@ -250,8 +251,8 @@
             vmem((n, rows, outs), bf),
             vmem((n, rows, outs), bf),
             dma((2 * chunks,)), dma((chunks,)), dma, dma((n,)), dma((n,)),
-            dma, dma((units,)), dma, dma((units,)),
-            dma, dma((units,)), dma, dma((units,)), dma((n,)), dma((n,)),
+            dma, dma((RING,)), dma, dma((RING,)),
+            dma, dma((RING,)), dma, dma((RING,)), dma((n,)), dma((n,)),
         ],
         compiler_params=pltpu.CompilerParams(
             collective_id=0, has_side_effects=True, vmem_limit_bytes=60 * 1024 * 1024),

time: 47 us -> 46.4 us (0.987)
  Pallas kernels: 46.2 us -> 45.6 us
    pallas_call x1, Pallas kernels: 46.2 us -> 45.6 us  [fused(): pl.pallas_call(functools.partial(kernel, n, chunks, width), out_shape=plt...]
where the time goes in v3:
time: 46.4 us; the launch traced here: 46.3 us
  Pallas kernels  45.6 us (98%)
  local copies, waits for them, and re-layouts  0.66 us (1%)
    pallas_call x1, Pallas kernels, fused(): pl.pallas_call(functools.partial(kernel, n, chunks, width), out_shape=plt...  45.6 us

profile of v3, /device:TPU:0, one launch (start us, length us, event | category | flops | bytes accessed | tf_op | source)
XLA Modules:
  0.0 46.3 jit_solution(17928782945142510258)
XLA Ops:
  0.0 45.6 %shard_map.46 = bf16[64,1024]{1,0:T(8,128)(2,1)S(1)} custom-call(bf16[64,1024]{1,0:T(8,128)(2,1)} %tokens.1, bf16[1024,3584]{1,0:T(8,128)(2,1)} %gate_w.1, bf16[1024,3584]{1,0:T(8,128)(2,1)} %up_w.1, bf16[3584,1024]{1,0:T(8,128)(2,1)} %down_w.1), custom_call_target="tpu_custom_call" | custom-call | tf_op jit(solution)/shard_map/pallas_call | solution.py:234
  45.6 0.7 %copy.6 = bf16[64,1024]{1,0:T(8,128)(2,1)} copy(bf16[64,1024]{1,0:T(8,128)(2,1)S(1)} %shard_map.46) | data formatting | bytes 262144

commit v4 on v3

--- a/solution.py
+++ b/solution.py
@@ -8,12 +8,13 @@
 from jax.sharding import PartitionSpec as P
 
 MESH = pl.DeviceIdType.MESH
-LAGS = (0, 3, 6, 9, 11)
-HEAD = 5
-NEAR = (4, 0)
+LAGS = (0, 3, 6, 9, 10)
+HEAD = (4, 5)
+NEAR = (5, 0)
 LAUNCH = (5, 9)
 DOWN_AT = 6
-RING = 12
+RING = 11
+FIRST, DEEP = 2, 4
 
 
 def flip(index, mask):
@@ -43,9 +44,9 @@
     their_half = pl.ds(pl.multiple_of((1 - b) * half, half), half)
     sent = [my_rows, chip_rows, span(1 - b, a), span(1 - b, 1 - a)]
     units = n * chunks
-    head = min(HEAD, chunks)
-    ahead = chunks - head
+    ahead = chunks - min(max(HEAD), chunks)
     outer = jnp.logical_or(z == 0, z == n - 1)
+    head = jnp.where(outer, *[min(count, chunks) for count in HEAD])
     near = jnp.where(outer, *[min(count, chunks - 1) for count in NEAR])
     launch = jnp.where(outer, *LAUNCH)
     filled = head + near
@@ -68,7 +69,7 @@
         pltpu.make_async_copy(gate_w.at[:, columns(k)], gate_v.at[k], w_sem.at[2 * k]).start()
         pltpu.make_async_copy(up_w.at[:, columns(k)], up_v.at[k], w_sem.at[2 * k + 1]).start()
 
-    for j in range(min(2, chunks)):
+    for j in range(min(FIRST, chunks)):
         load((ahead + j) % chunks)
 
     barrier = pltpu.get_barrier_semaphore()
@@ -105,6 +106,8 @@
         own.wait()
         for s in range(1, max(n - 1, 2)):
             tok_copy(s).start()
+        for j in range(min(FIRST, chunks), min(DEEP, chunks)):
+            load((ahead + j) % chunks)
 
     def ready(t):
         s, k = place(t)
@@ -148,9 +151,9 @@
     def step(offsets, loads, t, carry):
         dot, red, act, fwd, dwn = [None if o is None else t + o for o in offsets]
         if dot is not None:
-            @pl.when(dot + 2 < chunks)
-            def _():
-                load(lax.rem(dot + ahead + 2, chunks))
+            @pl.when(dot + DEEP < chunks)
+            def _():
+                load(lax.rem(dot + ahead + DEEP, chunks))
         if loads:
             @pl.when(jnp.logical_and(t >= DOWN_AT, t < chunks + DOWN_AT))
             def _():

time: 46.4 us -> 46.5 us (level)
  no operation moved by 1% of the time
where the time goes in v4:
time: 46.5 us; the launch traced here: 46.3 us
  Pallas kernels  45.7 us (98%)
  local copies, waits for them, and re-layouts  0.66 us (1%)
    pallas_call x1, Pallas kernels, fused(): pl.pallas_call(functools.partial(kernel, n, chunks, width), out_shape=plt...  45.7 us

profile of v4, /device:TPU:0, one launch (start us, length us, event | category | flops | bytes accessed | tf_op | source)
XLA Modules:
  0.0 46.3 jit_solution(14576123118703447782)
XLA Ops:
  0.0 45.7 %shard_map.46 = bf16[64,1024]{1,0:T(8,128)(2,1)S(1)} custom-call(bf16[64,1024]{1,0:T(8,128)(2,1)} %tokens.1, bf16[1024,3584]{1,0:T(8,128)(2,1)} %gate_w.1, bf16[1024,3584]{1,0:T(8,128)(2,1)} %up_w.1, bf16[3584,1024]{1,0:T(8,128)(2,1)} %down_w.1), custom_call_target="tpu_custom_call" | custom-call | tf_op jit(solution)/shard_map/pallas_call | solution.py:237
  45.7 0.7 %copy.6 = bf16[64,1024]{1,0:T(8,128)(2,1)} copy(bf16[64,1024]{1,0:T(8,128)(2,1)S(1)} %shard_map.46) | data formatting | bytes 262144
